TPU v7x, 512 devices: a 4x2x32 block of a 4x8x32 slice. The times are simulated.
512 devices in a mesh: crops: 2 (over y), dap: 64 (over z, core), chan: 4 (over x).
Axes of the slice: x: 4, y: 2, z: 32, core: 2. Of those that a mesh axis runs over, the one named last changes fastest.
The devices are a block of a 4x8x32 slice.
Arguments:
- prior_pair: bfloat16 [512, 256, 128], P(('crops', 'dap')), parts along dimension 0, may hold values from -12 to 12
- single: bfloat16 [512, 384], P(('crops', 'dap')), parts along dimension 0, may hold values from -6 to 6
- target: int32 [512], P(('crops', 'dap')), parts along dimension 0, may hold values from 0 to 21
- residue_mask: int32 [512], P(('crops', 'dap')), parts along dimension 0, may hold values 0 or 1
- recycle_gain: float32 [128], replicated, may hold values from 0.5 to 1.5
- recycle_bias: float32 [128], replicated, may hold values from -3 to 3
- left_single: bfloat16 [384, 128], replicated, may hold values from -0.3125 to 0.3125
- right_single: bfloat16 [384, 128], replicated, may hold values from -0.3125 to 0.3125
- left_target: bfloat16 [22, 128], replicated, may hold values from -3 to 3
- right_target: bfloat16 [22, 128], replicated, may hold values from -3 to 3
- tri_gain: float32 [2, 128], replicated, may hold values from 0.25 to 1.75
- tri_proj: bfloat16 [2, 128, 4, 128], replicated, may hold values from -0.5 to 0.5
- tri_gate: bfloat16 [2, 128, 128], replicated, may hold values from -0.5 to 0.5
- tri_gate_bias: float32 [2, 128], replicated, may hold values from -4 to 4
- tri_out_gain: float32 [2, 128], replicated, may hold values from 0.25 to 1.75
- tri_out: bfloat16 [2, 128, 128], replicated, may hold values from -0.5 to 0.5
Outputs:
- updated_pair: bfloat16 [512, 256, 128], P(('crops', 'dap')), parts along dimension 0
There are 2 independent parts, one for each index of `crops`. A program takes and returns all parts, laid end to end along the dimension named above; an argument that names none is the same for every part. Nothing has to cross between parts.
All inputs are finite; a program needn't handle non-finite values. No bound on the sum of `residue_mask` on one device may be relied on, other than what follows from the above.
Results may differ from a plain program's by a relative error of at most 0.0085.
Values may be sent and summed in bfloat16 or wider, within the bound.
A program may use at most 64 MiB of HBM per device.

v0:
```python
import math
import jax
import jax.numpy as jnp
from jax import lax
from jax.sharding import PartitionSpec as P


def side_by_side(arrays, axis, dim, along):
    widths = [math.prod(a.shape[along:]) for a in arrays]
    both = jnp.concatenate(
        [a.reshape(*a.shape[:along], w) for a, w in zip(arrays, widths)], axis=along
    )
    out = lax.all_gather(both, axis, axis=dim, tiled=True)
    blocks = jnp.split(out, [sum(widths[:k]) for k in range(1, len(widths))], axis=along)
    return tuple((b.reshape(*out.shape[:along], *a.shape[along:]) for a, b in zip(arrays, blocks)))


def in_order(blocks, dim):
    lengths = list(blocks.shape[1:])
    lengths[dim] *= blocks.shape[0]
    return jnp.moveaxis(blocks, 0, dim).reshape(lengths)


def copy_for_each(shard, axis):
    peers = lax.axis_size(axis)
    return lax.all_to_all(
        jnp.broadcast_to(shard[None], (peers, *shard.shape)), axis, 0, 0, tiled=True
    )


def gathered_copies(shard, axis, dim):
    return in_order(copy_for_each(shard, axis), dim)


def layer_norm(values, axis):
    center = values - jnp.mean(values, axis=axis, keepdims=True)
    spread = jnp.mean(center * center, axis=axis, keepdims=True)
    return center * lax.rsqrt(spread + 1e-05)


def gated_edges(projected, mask_block):
    masked = mask_block[:, :, None]
    first = (masked * jax.nn.sigmoid(projected[:, :, 1]) * projected[:, :, 0]).astype(jnp.bfloat16)
    second = (masked * jax.nn.sigmoid(projected[:, :, 3]) * projected[:, :, 2]).astype(jnp.bfloat16)
    return (jnp.transpose(first, (2, 0, 1)), jnp.transpose(second, (2, 0, 1)))


def body(
    prior_pair,
    single,
    target,
    residue_mask,
    recycle_gain,
    recycle_bias,
    left_single,
    right_single,
    left_target,
    right_target,
    tri_gain,
    tri_proj,
    tri_gate,
    tri_gate_bias,
    tri_out_gain,
    tri_out,
):
    row_count, col_count, depth = prior_pair.shape
    hidden_width = tri_proj.shape[3]
    mask_float = residue_mask.astype(jnp.float32)
    one_hot = (
        target[:, None] == jnp.arange(left_target.shape[0], dtype=jnp.int32)[None, :]
    ).astype(jnp.bfloat16)
    left_terms = jnp.dot(single, left_single, preferred_element_type=jnp.float32) + jnp.dot(
        one_hot, left_target, preferred_element_type=jnp.float32
    )
    right_terms = jnp.dot(single, right_single, preferred_element_type=jnp.float32) + jnp.dot(
        one_hot, right_target, preferred_element_type=jnp.float32
    )
    right_whole, mask_whole = side_by_side((right_terms, mask_float), "dap", 0, 1)
    pair_mask = mask_float[:, None] * mask_whole[None, :]
    prior_norm = layer_norm(prior_pair.astype(jnp.float32), 2) * recycle_gain + recycle_bias
    pair_state = (prior_norm + left_terms[:, None, :] + right_whole[None, :, :]).astype(
        jnp.bfloat16
    )
    groups = lax.axis_size("chan")
    member = lax.axis_index("chan")
    local_width = hidden_width // groups

    def local_edges(flat_normed, weights):
        weights_local = lax.dynamic_slice_in_dim(weights, member * local_width, local_width, 2)
        projected = jnp.dot(
            flat_normed,
            weights_local.reshape(depth, 4 * local_width),
            preferred_element_type=jnp.float32,
        )
        return gated_edges(projected.reshape(row_count, col_count, 4, local_width), pair_mask)

    for layer in range(2):
        normed = (layer_norm(pair_state.astype(jnp.float32), 2) * tri_gain[layer]).astype(
            jnp.bfloat16
        )
        flat_normed = normed.reshape(-1, depth)
        if layer == 0:
            outgoing_left_edges, outgoing_right_edges = local_edges(flat_normed, tri_proj[layer])
            product = jnp.einsum(
                "cik,cjk->cij",
                outgoing_left_edges,
                lax.all_gather(outgoing_right_edges, "dap", axis=1, tiled=True),
                preferred_element_type=jnp.float32,
            )
        else:
            left_edges, right_edges = local_edges(flat_normed, tri_proj[layer])
            transposed = lax.all_to_all(left_edges, "dap", split_axis=2, concat_axis=1, tiled=True)
            product = jnp.einsum(
                "cki,ckj->cij",
                transposed,
                lax.all_gather(right_edges, "dap", axis=1, tiled=True),
                preferred_element_type=jnp.float32,
            )
        full_product = gathered_copies(product.astype(jnp.bfloat16), "chan", 0)
        normed_hidden = (
            layer_norm(full_product.astype(jnp.float32), 0) * tri_out_gain[layer][:, None, None]
        ).astype(jnp.bfloat16)
        update = jnp.einsum(
            "cij,cd->ijd", normed_hidden, tri_out[layer], preferred_element_type=jnp.float32
        )
        gating = jax.nn.sigmoid(
            jnp.dot(flat_normed, tri_gate[layer], preferred_element_type=jnp.float32)
            + tri_gate_bias[layer]
        )
        pair_state = (
            pair_state.astype(jnp.float32) + gating.reshape(row_count, col_count, depth) * update
        ).astype(jnp.bfloat16)
    return pair_state


def solution(mesh):
    placed = (
        P(("crops", "dap"), None, None),
        P(("crops", "dap"), None),
        P(("crops", "dap")),
        P(("crops", "dap")),
        P(),
        P(),
        P(),
        P(),
        P(),
        P(),
        P(),
        P(),
        P(),
        P(),
        P(),
        P(),
    )
    return jax.shard_map(
        body, mesh=mesh, in_specs=placed, out_specs=P(("crops", "dap"), None, None), check_vma=False
    )
```

profile of v0, /device:TPU:33, one launch (start us, length us, event | category | flops | bytes accessed | tf_op | source)
XLA Modules:
  0.0 407.9 jit_solution(16664484103935328032)
XLA Ops:
  7.4 0.8 fusion.102
  8.3 0.9 convolution_add_fusion.2
  9.2 97.4 %all-gather = f32[64,4,129]{2,1,0:T(4,128)S(1)} all-gather(f32[1,4,129]{2,1,0:T(4,128)S(1)} %maximum_bitcast_fusion), channel_id=1, replica_groups=mesh['crops'=2,'dap'=64,'chan'=4] {'dap'}, dimensions={0}, use_global_device_ids=true | all-gather | bytes 134160 | tf_op jit(solution)/shard_map/all_gather | solution.py:13
  106.8 1.1 convert_reduce_fusion.3
  107.9 1.3 fusion.40
  109.2 1.0 fusion.101
  110.3 0.9 convolution_add_fusion.3
  111.2 1.5 convert_reduce_fusion
  113.1 0.8 slice_bitcast_fusion.7
  113.8 1.1 fusion.98
  116.9 121.3 %all-gather.4.cloned.1.call-done = bf16[32,256,256]{2,0,1:T(8,128)(2,1)} async-done(((bf16[32,4,256]{2,0,1:T(8,128)(2,1)}), bf16[32,256,256]{2,0,1:T(8,128)(2,1)}) %all-gather.4.cloned.1.call-update) | async-done | bytes 4194320 | tf_op jit(solution)/shard_map/all_gather | solution.py:107
  238.2 4.5 %fusion.17 = bf16[32,4,256]{2,1,0:T(4,128)(2,1)S(1)} fusion(bf16[32,256,256]{2,0,1:T(8,128)(2,1)} %all-gather.4.cloned.1.call-done, bf16[32,4,256]{2,0,1:T(8,128)(2,1)S(1)} %get-tuple-element.11), kind=kOutput, calls=%fused_computation.21 | convolution fusion | flops 16809984 | bytes 4325376 | tf_op jit(solution)/shard_map/cik,cjk->cij/dot_general | solution.py:104
  242.8 0.7 broadcast_in_dim.4
  243.5 4.0 all-to-all-start
  247.8 5.6 %all-to-all-done = bf16[4,32,4,256]{3,1,2,0:T(8,128)(2,1)S(1)} async-done(((bf16[4,32,4,256]{3,1,2,0:T(8,128)(2,1)}), bf16[4,32,4,256]{3,1,2,0:T(8,128)(2,1)S(1)}, u32[]{:S(2)}, u32[]{:S(2)}) %all-to-all-start) | async-done | bytes 262176 | tf_op jit(solution)/shard_map/all_to_all | solution.py:26
  256.0 0.8 reshape.193
  256.8 14.6 %all-to-all-start.1 = ((bf16[64,2,256]{2,1,0:T(2,128)(2,1)}), bf16[64,2,256]{2,1,0:T(2,128)(2,1)S(1)}, u32[]{:S(2)}, u32[]{:S(2)}) async-start(bf16[64,2,256]{2,1,0:T(2,128)(2,1)} %reshape.193), calls=%async_computation.1 | async-start | bytes 131072 | tf_op jit(solution)/shard_map/all_to_all | solution.py:112
  271.6 24.9 %all-to-all-done.1 = bf16[64,2,256]{2,1,0:T(2,128)(2,1)S(1)} async-done(((bf16[64,2,256]{2,1,0:T(2,128)(2,1)}), bf16[64,2,256]{2,1,0:T(2,128)(2,1)S(1)}, u32[]{:S(2)}, u32[]{:S(2)}) %all-to-all-start.1) | async-done | bytes 65568 | tf_op jit(solution)/shard_map/all_to_all | solution.py:112
  297.1 87.5 %all-gather.6.cloned.1.call-done = bf16[32,256,256]{2,0,1:T(8,128)(2,1)} async-done(((bf16[32,4,256]{2,0,1:T(8,128)(2,1)}), bf16[32,256,256]{2,0,1:T(8,128)(2,1)}) %all-gather.6.cloned.1.call-update) | async-done | bytes 4194320 | tf_op jit(solution)/shard_map/all_gather | solution.py:116
  384.6 4.5 %fusion.20 = bf16[32,4,256]{2,1,0:T(4,128)(2,1)S(1)} fusion(bf16[32,256,4]{1,2,0:T(4,128)(2,1)S(1)} %copy.69, bf16[32,256,256]{2,0,1:T(8,128)(2,1)} %all-gather.6.cloned.1.call-done), kind=kOutput, calls=%fused_computation.22 | convolution fusion | flops 16809984 | bytes 4325376 | tf_op jit(solution)/shard_map/cki,ckj->cij/dot_general | solution.py:113
  389.1 0.7 broadcast_in_dim.5
  389.9 4.1 all-to-all-start.2
  394.2 5.6 %all-to-all-done.2 = bf16[4,32,4,256]{3,1,2,0:T(8,128)(2,1)S(1)} async-done(((bf16[4,32,4,256]{3,1,2,0:T(8,128)(2,1)}), bf16[4,32,4,256]{3,1,2,0:T(8,128)(2,1)S(1)}, u32[]{:S(2)}, u32[]{:S(2)}) %all-to-all-start.2) | async-done | bytes 262176 | tf_op jit(solution)/shard_map/all_to_all | solution.py:26
  400.1 1.0 fusion.14
  (62 shorter events, 7.5 us)
Async XLA Ops:
  6.5 0.9 copy-start
  6.6 110.1 %copy-start.2 = (f32[2,128]{1,0:T(2,128)S(1)}, f32[2,128]{1,0:T(2,128)}, u32[]{:S(2)}) copy-start(f32[2,128]{1,0:T(2,128)} %param.30) | copy-start | bytes 3076
  6.6 110.3 %copy-start.3 = (f32[2,128]{1,0:T(2,128)S(1)}, f32[2,128]{1,0:T(2,128)}, u32[]{:S(2)}) copy-start(f32[2,128]{1,0:T(2,128)} %param.29) | copy-start | bytes 3076
  6.6 231.6 %all-gather.4.cloned.1.call-start = ((), (), s32[]{:S(2)}) async-start(), calls=%async_computation.3 | async-start | bytes 4259840 | tf_op jit(solution)/shard_map/all_gather | solution.py:107
  114.9 132.6 %copy-start.4 = (bf16[2,128,128]{2,1,0:T(8,128)(2,1)S(1)}, bf16[2,128,128]{2,1,0:T(8,128)(2,1)}, u32[]{:S(2)}) copy-start(bf16[2,128,128]{2,1,0:T(8,128)(2,1)} %param.28) | copy-start | bytes 196612
  238.2 15.5 %copy-start.1 = (bf16[2,128,128]{2,1,0:T(8,128)(2,1)S(1)}, bf16[2,128,128]{2,1,0:T(8,128)(2,1)}, u32[]{:S(2)}) copy-start(bf16[2,128,128]{2,1,0:T(8,128)(2,1)} %param.31) | copy-start | bytes 196612
  243.5 9.9 %all-to-all-start = ((bf16[4,32,4,256]{3,1,2,0:T(8,128)(2,1)}), bf16[4,32,4,256]{3,1,2,0:T(8,128)(2,1)S(1)}, u32[]{:S(2)}, u32[]{:S(2)}) async-start(bf16[4,32,4,256]{3,1,2,0:T(8,128)(2,1)} %broadcast_in_dim.4), calls=%async_computation | async-start | bytes 524288 | tf_op jit(solution)/shard_map/all_to_all | solution.py:26
  247.5 137.1 %all-gather.6.cloned.1.call-start = ((), (), s32[]{:S(2)}) async-start(), calls=%async_computation.4 | async-start | bytes 4259840 | tf_op jit(solution)/shard_map/all_gather | solution.py:116
  256.8 39.6 %all-to-all-start.1 = ((bf16[64,2,256]{2,1,0:T(2,128)(2,1)}), bf16[64,2,256]{2,1,0:T(2,128)(2,1)S(1)}, u32[]{:S(2)}, u32[]{:S(2)}) async-start(bf16[64,2,256]{2,1,0:T(2,128)(2,1)} %reshape.193), calls=%async_computation.1 | async-start | bytes 131072 | tf_op jit(solution)/shard_map/all_to_all | solution.py:112
  389.9 10.0 %all-to-all-start.2 = ((bf16[4,32,4,256]{3,1,2,0:T(8,128)(2,1)}), bf16[4,32,4,256]{3,1,2,0:T(8,128)(2,1)S(1)}, u32[]{:S(2)}, u32[]{:S(2)}) async-start(bf16[4,32,4,256]{3,1,2,0:T(8,128)(2,1)} %broadcast_in_dim.5), calls=%async_computation.2 | async-start | bytes 524288 | tf_op jit(solution)/shard_map/all_to_all | solution.py:26
Sparse Core Ops, SparseCore 0:
  116.8 121.3 all-gather.3
  255.9 128.6 all-gather.5
where the time goes:
time: 409 us; the launch traced here: 408 us
  waiting for transfers between devices  245 us (60%)
  blocking collectives  97.4 us (24%)
  starting transfers between devices  22.7 us (6%)
  matrix products  15.1 us (4%)
  between operations  13.7 us (3%)
  other arithmetic  8.15 us (2%)
  local copies, waits for them, and re-layouts  5.89 us (1%)
    all_gather x1, waiting for transfers between devices, body(): lax.all_gather(outgoing_right_edges, 'dap', axis=1, tiled=True)  121 us
    all_gather x1, blocking collectives, side_by_side(): out = lax.all_gather(both, axis, axis=dim, tiled=True)  97.4 us
    all_gather x1, waiting for transfers between devices, body(): lax.all_gather(right_edges, 'dap', axis=1, tiled=True)  87.5 us
    all_to_all x1, waiting for transfers between devices, body(): lax.all_to_all(left_edges, 'dap', split_axis=2, concat_axis=1, tiled=True)  24.9 us
    all_to_all x1, starting transfers between devices, body(): lax.all_to_all(left_edges, 'dap', split_axis=2, concat_axis=1, tiled=True)  14.6 us
    all_to_all x2, waiting for transfers between devices, copy_for_each(): lax.all_to_all(jnp.broadcast_to(shard[None], (peers, *shard.shape)), axis...  11.2 us
  transfers between devices with their start and end apart: 5, of which 5 were waited for; matrix products, arithmetic and copies ran while one was open for 1% of the time, Pallas kernels for 0%

commit v1 on v0

--- a/solution.py
+++ b/solution.py
@@ -104,7 +104,12 @@
             product = jnp.einsum(
                 "cik,cjk->cij",
                 outgoing_left_edges,
-                lax.all_gather(outgoing_right_edges, "dap", axis=1, tiled=True),
+                jnp.concatenate(
+                    lax.all_to_all(
+                        jnp.stack([outgoing_right_edges] * lax.axis_size("dap")), "dap", 0, 0
+                    ),
+                    axis=1,
+                ),
                 preferred_element_type=jnp.float32,
             )
         else:

time: 409 us -> 681 us (1.67)
  waiting for transfers between devices: 245 us -> 495 us
  local copies, waits for them, and re-layouts: 5.89 us -> 23.2 us
    all_to_all x0 -> x1, waiting for transfers between devices: none -> 372 us  [body(): lax.all_to_all(jnp.stack([outgoing_right_edges] * lax.axis_size('dap')),...]
    all_gather x1 -> x0, waiting for transfers between devices: 121 us -> none  [body(): lax.all_gather(outgoing_right_edges, 'dap', axis=1, tiled=True)]
    reshape x0 -> x2, local copies, waits for them, and re-layouts: none -> 13.3 us  [body(): jnp.concatenate(lax.all_to_all(jnp.stack([outgoing_right_edges] * lax.axi...]
  transfers between devices with their start and end apart: 5 -> 5, of which waited for: 5 -> 5; matrix products, arithmetic and copies ran while one was open for 1% -> 0% of each run, Pallas kernels for 0% -> 0%
where the time goes in v1:
time: 681 us; the launch traced here: 680 us
  waiting for transfers between devices  495 us (73%)
  blocking collectives  97.4 us (14%)
  starting transfers between devices  28.8 us (4%)
  local copies, waits for them, and re-layouts  23.2 us (3%)
  matrix products  13.9 us (2%)
  between operations  13.7 us (2%)
  other arithmetic  7.52 us (1%)
    all_to_all x1, waiting for transfers between devices, body(): lax.all_to_all(jnp.stack([outgoing_right_edges] * lax.axis_size('dap')),...  372 us
    all_gather x1, blocking collectives, side_by_side(): out = lax.all_gather(both, axis, axis=dim, tiled=True)  97.4 us
    all_gather x1, waiting for transfers between devices, body(): lax.all_gather(right_edges, 'dap', axis=1, tiled=True)  85.9 us
    all_to_all x1, waiting for transfers between devices, body(): lax.all_to_all(left_edges, 'dap', split_axis=2, concat_axis=1, tiled=True)  26.7 us
    all_to_all x1, starting transfers between devices, body(): lax.all_to_all(left_edges, 'dap', split_axis=2, concat_axis=1, tiled=True)  14.7 us
  transfers between devices with their start and end apart: 5, of which 5 were waited for; matrix products, arithmetic and copies ran while one was open for 0% of the time, Pallas kernels for 0%

profile of v1, /device:TPU:33, one launch (start us, length us, event | category | flops | bytes accessed | tf_op | source)
XLA Modules:
  0.0 679.8 jit_solution(3352724007458941109)
XLA Ops:
  8.3 0.9 convolution_add_fusion.2
  9.2 97.4 %all-gather = f32[64,4,129]{2,1,0:T(4,128)S(1)} all-gather(f32[1,4,129]{2,1,0:T(4,128)S(1)} %maximum_bitcast_fusion), channel_id=1, replica_groups=mesh['crops'=2,'dap'=64,'chan'=4] {'dap'}, dimensions={0}, use_global_device_ids=true | all-gather | bytes 134160 | tf_op jit(solution)/shard_map/all_gather | solution.py:13
  106.8 1.1 convert_reduce_fusion.3
  107.9 1.3 fusion.35
  109.2 1.0 fusion.96
  110.3 0.9 convolution_add_fusion.3
  111.2 1.5 convert_reduce_fusion
  113.9 1.1 fusion.93
  116.0 4.0 stack.2
  120.0 6.2 all-to-all-start
  126.5 371.8 %all-to-all-done = bf16[64,32,4,256]{3,2,1,0:T(4,128)(2,1)} async-done(((bf16[64,32,4,256]{3,2,1,0:T(4,128)(2,1)}), bf16[64,32,4,256]{3,2,1,0:T(4,128)(2,1)}, u32[]{:S(2)}, u32[]{:S(2)}) %all-to-all-start) | async-done | bytes 4194336 | tf_op jit(solution)/shard_map/all_to_all | solution.py:108
  498.3 6.3 copy.57
  504.6 6.9 %reshape.178 = bf16[32,256,256]{2,1,0:T(8,128)(2,1)} reshape(bf16[32,64,4,256]{3,2,1,0:T(4,128)(2,1)} %copy.57) | data formatting | bytes 8388608 | tf_op jit(solution)/shard_map/reshape | solution.py:107
  511.5 3.4 convolution_convert_fusion
  515.7 4.3 all-to-all-start.1
  520.3 5.2 all-to-all-done.1
  528.2 0.8 reshape.203
  529.0 14.7 %all-to-all-start.2 = ((bf16[64,2,256]{2,1,0:T(2,128)(2,1)}), bf16[64,2,256]{2,1,0:T(2,128)(2,1)S(1)}, u32[]{:S(2)}, u32[]{:S(2)}) async-start(bf16[64,2,256]{2,1,0:T(2,128)(2,1)} %reshape.203), calls=%async_computation.2 | async-start | bytes 131072 | tf_op jit(solution)/shard_map/all_to_all | solution.py:117
  543.8 26.7 %all-to-all-done.2 = bf16[64,2,256]{2,1,0:T(2,128)(2,1)S(1)} async-done(((bf16[64,2,256]{2,1,0:T(2,128)(2,1)}), bf16[64,2,256]{2,1,0:T(2,128)(2,1)S(1)}, u32[]{:S(2)}, u32[]{:S(2)}) %all-to-all-start.2) | async-done | bytes 65568 | tf_op jit(solution)/shard_map/all_to_all | solution.py:117
  571.1 85.9 %all-gather.3.cloned.1.call-done = bf16[32,256,256]{2,0,1:T(8,128)(2,1)} async-done(((bf16[32,4,256]{2,0,1:T(8,128)(2,1)}), bf16[32,256,256]{2,0,1:T(8,128)(2,1)}) %all-gather.3.cloned.1.call-update) | async-done | bytes 4194320 | tf_op jit(solution)/shard_map/all_gather | solution.py:121
  657.0 4.5 fusion.15
  662.3 3.5 all-to-all-start.3
  666.1 5.6 all-to-all-done.3
  672.0 1.0 fusion.12
  (65 shorter events, 10.0 us)
Async XLA Ops:
  6.5 0.9 copy-start
  120.0 6.2 copy-start.2
  120.0 6.4 copy-start.3
  120.0 378.2 %all-to-all-start = ((bf16[64,32,4,256]{3,2,1,0:T(4,128)(2,1)}), bf16[64,32,4,256]{3,2,1,0:T(4,128)(2,1)}, u32[]{:S(2)}, u32[]{:S(2)}) async-start(bf16[64,32,4,256]{3,2,1,0:T(4,128)(2,1)} %stack.2), calls=%async_computation | async-start | bytes 8388608 | tf_op jit(solution)/shard_map/all_to_all | solution.py:108
  511.5 8.5 %copy-start.4 = (bf16[2,128,128]{2,1,0:T(8,128)(2,1)S(1)}, bf16[2,128,128]{2,1,0:T(8,128)(2,1)}, u32[]{:S(2)}) copy-start(bf16[2,128,128]{2,1,0:T(8,128)(2,1)} %param.28) | copy-start | bytes 196612
  511.5 14.3 %copy-start.1 = (bf16[2,128,128]{2,1,0:T(8,128)(2,1)S(1)}, bf16[2,128,128]{2,1,0:T(8,128)(2,1)}, u32[]{:S(2)}) copy-start(bf16[2,128,128]{2,1,0:T(8,128)(2,1)} %param.31) | copy-start | bytes 196612
  515.7 9.8 %all-to-all-start.1 = ((bf16[4,32,4,256]{3,1,2,0:T(8,128)(2,1)}), bf16[4,32,4,256]{3,1,2,0:T(8,128)(2,1)S(1)}, u32[]{:S(2)}, u32[]{:S(2)}) async-start(bf16[4,32,4,256]{3,1,2,0:T(8,128)(2,1)} %broadcast_in_dim.4), calls=%async_computation.1 | async-start | bytes 524288 | tf_op jit(solution)/shard_map/all_to_all | solution.py:26
  520.0 137.0 %all-gather.3.cloned.1.call-start = ((), (), s32[]{:S(2)}) async-start(), calls=%async_computation.4 | async-start | bytes 4259840 | tf_op jit(solution)/shard_map/all_gather | solution.py:121
  529.0 41.5 %all-to-all-start.2 = ((bf16[64,2,256]{2,1,0:T(2,128)(2,1)}), bf16[64,2,256]{2,1,0:T(2,128)(2,1)S(1)}, u32[]{:S(2)}, u32[]{:S(2)}) async-start(bf16[64,2,256]{2,1,0:T(2,128)(2,1)} %reshape.203), calls=%async_computation.2 | async-start | bytes 131072 | tf_op jit(solution)/shard_map/all_to_all | solution.py:117
  662.3 9.4 %all-to-all-start.3 = ((bf16[4,32,4,256]{3,1,2,0:T(8,128)(2,1)}), bf16[4,32,4,256]{3,1,2,0:T(8,128)(2,1)S(1)}, u32[]{:S(2)}, u32[]{:S(2)}) async-start(bf16[4,32,4,256]{3,1,2,0:T(8,128)(2,1)} %broadcast_in_dim.5), calls=%async_computation.3 | async-start | bytes 524288 | tf_op jit(solution)/shard_map/all_to_all | solution.py:26
Sparse Core Ops, SparseCore 0:
  528.1 128.8 all-gather.2
